TPU v7x, 32 devices: a whole 2x2x4 slice. The times are simulated.
32 devices in a mesh: grp: 2 (over y), row: 4 (over z), col: 2 (over x), cls: 2 (over core).
Axes of the slice: x: 2, y: 2, z: 4, core: 2. Of those that a mesh axis runs over, the one named last changes fastest.
Arguments:
- unary_scores: int32 [32, 16, 256], P('cls', ('grp', 'row'), 'col'), parts along dimension 1, may hold values from -256 to 256
- confidence: float32 [16, 256], P(('grp', 'row'), 'col'), parts along dimension 0, may hold values from 0.5 to 64
- features: bfloat16 [16, 256, 256], P(('grp', 'row'), 'col'), parts along dimension 0, may hold values from -12 to 12
- compat_table: int32 [32, 32], replicated, may hold values from 0 to 7
Outputs:
- belief: bfloat16 [32, 16, 256], P('cls', ('grp', 'row'), 'col'), parts along dimension 1
There are 2 independent parts, one for each index of `grp`. A program takes and returns all parts, laid end to end along the dimension named above; an argument that names none is the same for every part. Nothing has to cross between parts.
All inputs are finite; a program needn't handle non-finite values.
Results may differ from a plain program's by a relative error of at most 0.0021.
Values may be sent and summed in bfloat16 or wider, within the bound.
A program may use at most 64 MiB of HBM per device.

v0:
```python
import jax
import jax.numpy as jnp
from jax import lax
from jax.sharding import PartitionSpec as P

LIVE = 21
unit_scale = 1.0 / 64.0
masked_low = -1e30
key_block = 1024


def class_softmax(logits, live_mask):
    class_top = jnp.max(jnp.where(live_mask, logits, masked_low), axis=0)
    raised = jnp.where(live_mask, jnp.exp(logits - class_top[None]), 0.0)
    return raised / jnp.sum(raised, axis=0)[None]


def make_fold(query_feats, query_norm, query_ids, key_ids, feat_depth):

    def add_block(running, key_piece, beliefs, key_start):
        key_count = key_piece.shape[1]
        scores = jnp.dot(query_feats, key_piece, preferred_element_type=jnp.float32)
        key_norm = jnp.sum(jnp.square(key_piece.astype(jnp.float32)), axis=0)
        spread = (query_norm[:, None] + key_norm[None, :] - 2.0 * scores) * (2.0 / feat_depth)
        same_pixel = query_ids[:, None] == key_ids(key_start, key_count)[None, :]
        kernel = jnp.where(same_pixel, 0.0, jnp.exp(4.0 - spread)).astype(jnp.bfloat16)
        return running + lax.dot_general(
            beliefs, kernel, (((1,), (1,)), ((), ())), preferred_element_type=jnp.float32
        )

    def fold_keys(running, pieces, key_start):
        key_piece, beliefs = pieces
        key_count = key_piece.shape[1]
        if key_count > key_block and key_count % key_block == 0:

            def block_step(block_index, running_sum):
                block_start = block_index * key_block
                return add_block(
                    running_sum,
                    lax.dynamic_slice_in_dim(key_piece, block_start, key_block, 1),
                    lax.dynamic_slice_in_dim(beliefs, block_start, key_block, 1),
                    key_start + block_start,
                )

            return lax.fori_loop(0, key_count // key_block, block_step, running)
        return add_block(running, key_piece, beliefs, key_start)

    return fold_keys


def body(unary_scores, confidence, features, compat_table):
    class_share, row_count, col_count = unary_scores.shape
    feat_depth = features.shape[2]
    cls_count = lax.axis_size("cls")
    col_groups = lax.axis_size("col")
    cls_index = lax.axis_index("cls")
    row_index = lax.axis_index("row")
    col_index = lax.axis_index("col")
    full_width = col_count * col_groups
    pixels = row_count * col_count
    half_cols = col_count // cls_count
    keys_local = row_count * half_cols
    whole_unary = lax.all_gather(unary_scores, "cls", axis=0, tiled=True)
    classes = whole_unary.shape[0]
    logits0 = confidence[None] * (whole_unary.astype(jnp.float32) * unit_scale)
    live_all = (lax.iota(jnp.int32, classes) < LIVE)[:, None, None]
    belief0 = class_softmax(logits0, live_all).astype(jnp.bfloat16)
    offset = cls_index * half_cols
    key_belief = lax.dynamic_slice_in_dim(belief0, offset, half_cols, 2).reshape(
        classes, keys_local
    )
    key_feats = (
        lax.dynamic_slice_in_dim(features, offset, half_cols, 1).reshape(keys_local, feat_depth).T
    )

    def spread_ids(key_start, key_count):
        key_place = key_start + lax.iota(jnp.int32, key_count)
        key_owner = key_place // keys_local
        within = key_place % keys_local
        global_row = key_owner // col_groups * row_count + within // half_cols
        global_col = key_owner % col_groups * col_count + offset + within % half_cols
        return global_row * full_width + global_col

    query_feats = features.reshape(pixels, feat_depth)
    query_norm = jnp.sum(jnp.square(query_feats.astype(jnp.float32)), axis=1)
    local_ids = lax.iota(jnp.int32, pixels)
    query_ids = (
        (row_index * row_count + local_ids // col_count) * full_width
        + col_index * col_count
        + local_ids % col_count
    )
    fold_own = make_fold(query_feats, query_norm, query_ids, spread_ids, feat_depth)
    zero_start = jnp.zeros((classes, pixels), jnp.float32)
    band_feats, band_belief = (
        lax.all_gather(key_feats, "col", axis=1, tiled=True),
        lax.all_gather(key_belief, "col", axis=1, tiled=True),
    )
    message = fold_own(
        zero_start,
        (
            lax.all_gather(band_feats, "row", axis=1, tiled=True),
            lax.all_gather(band_belief, "row", axis=1, tiled=True),
        ),
        jnp.int32(0),
    )
    message = message / (2.0 * pixels)
    potts_weight = compat_table.astype(jnp.float32) * (1.0 - jnp.eye(classes, dtype=jnp.float32))
    partial_value = jnp.dot(potts_weight, message, precision=lax.Precision.HIGHEST)
    pairwise = lax.psum(partial_value, "cls")
    logits1 = logits0.reshape(classes, pixels) - pairwise
    belief1 = class_softmax(logits1, live_all.reshape(classes, 1))
    own_belief = lax.dynamic_slice_in_dim(belief1, cls_index * class_share, class_share, 0)
    return own_belief.astype(jnp.bfloat16).reshape(class_share, row_count, col_count)


def solution(mesh):
    in_specs = (
        P("cls", ("grp", "row"), "col"),
        P(("grp", "row"), "col"),
        P(("grp", "row"), "col", None),
        P(),
    )
    out_specs = P("cls", ("grp", "row"), "col")
    return jax.shard_map(body, mesh=mesh, in_specs=in_specs, out_specs=out_specs, check_vma=False)
```

profile of v0, /device:TPU:0, one launch (start us, length us, event | category | flops | bytes accessed | tf_op | source)
XLA Modules:
  0.0 48.1 jit_solution(6375300446395197448)
XLA Ops:
  0.0 0.0 copy-start.2
  0.0 2.2 %all_gather.15 = s32[32,2,128]{2,1,0:T(2,128)S(1)} all-gather(s32[16,2,128]{2,1,0:T(2,128)} %param.4), channel_id=1, replica_groups=mesh['grp'=2,'row'=4,'col'=2,'cls'=2] {'cls'}, dimensions={0}, use_global_device_ids=true | all-gather | bytes 49152 | tf_op jit(solution)/shard_map/all_gather | solution.py:63
  2.2 0.0 copy-done.2
  2.2 0.1 select_reduce_fusion.1
  2.3 0.0 copy-start
  2.3 0.1 fusion.67
  2.4 0.1 constant_dynamic-slice_fusion.1
  2.5 0.1 fusion.19
  2.6 0.1 reshape.136
  2.7 5.1 %all_gather.16 = bf16[32,256]{1,0:T(8,128)(2,1)S(1)} all-gather(bf16[32,128]{1,0:T(8,128)(2,1)S(1)} %reshape.136), channel_id=1, replica_groups=mesh['grp'=2,'row'=4,'col'=2,'cls'=2] {'col'}, dimensions={1}, use_global_device_ids=true | all-gather | bytes 24576 | tf_op jit(solution)/shard_map/all_gather | solution.py:96
  7.8 14.0 %all_gather.17 = bf16[32,1024]{1,0:T(8,128)(2,1)S(1)} all-gather(bf16[32,256]{1,0:T(8,128)(2,1)S(1)} %all_gather.16), channel_id=1, replica_groups=mesh['grp'=2,'row'=4,'col'=2,'cls'=2] {'row'}, dimensions={1}, use_global_device_ids=true | all-gather | bytes 81920 | tf_op jit(solution)/shard_map/all_gather | solution.py:102
  21.8 0.0 copy-done
  21.8 4.9 %all_gather.18 = bf16[256,256]{0,1:T(8,128)(2,1)S(1)} all-gather(bf16[256,128]{0,1:T(8,128)(2,1)S(1)} %bitcast.38), channel_id=1, replica_groups=mesh['grp'=2,'row'=4,'col'=2,'cls'=2] {'col'}, dimensions={1}, use_global_device_ids=true | all-gather | bytes 196608 | tf_op jit(solution)/shard_map/all_gather | solution.py:95
  26.7 15.9 %all_gather.19 = bf16[256,1024]{0,1:T(8,128)(2,1)S(1)} all-gather(bf16[256,256]{0,1:T(8,128)(2,1)S(1)} %all_gather.18), channel_id=1, replica_groups=mesh['grp'=2,'row'=4,'col'=2,'cls'=2] {'row'}, dimensions={1}, use_global_device_ids=true | all-gather | bytes 655360 | tf_op jit(solution)/shard_map/all_gather | solution.py:101
  42.6 0.2 multiply_reduce_fusion
  42.9 0.1 multiply_reduce_fusion.1
  43.0 0.0 copy-start.1
  43.0 0.6 %fusion.8 = f32[32,256]{1,0:T(8,128)S(1)} fusion(bf16[32,1024]{1,0:T(8,128)(2,1)S(1)} %all_gather.17, bf16[256,1024]{0,1:T(8,128)(2,1)S(1)} %all_gather.19, bf16[256,256]{1,0:T(8,128)(2,1)S(1)} %bitcast.37, f32[1024]{0:T(1024)S(1)} %multiply_reduce_fusion, f32[256]{0:T(256)S(1)} %bitcast.39, s32[1024]{0:T(1024)S(1)} %fusion.36, s32[256]{0:T(256)S(1)} %fusion.57), kind=kOutput, calls=%fused_computation.9 | convolution fusion | flops 153100288 | bytes 763904 | tf_op jit(solution)/shard_map/dot_general | solution.py:27
  43.6 0.1 copy-done.1
  43.7 0.2 fusion.21
  43.9 3.4 %psum.7 = f32[32,256]{1,0:T(8,128)S(1)} all-reduce(f32[32,256]{1,0:T(8,128)S(1)} %fusion.21), channel_id=1, replica_groups=mesh['grp'=2,'row'=4,'col'=2,'cls'=2] {'cls'}, use_global_device_ids=true, to_apply=%region_4.5 | all-reduce | flops 8192 | bytes 65536 | tf_op jit(solution)/shard_map/psum | solution.py:109
  47.3 0.1 select_reduce_fusion
  47.4 0.1 fusion.66
  47.5 0.6 %reshape.139 = bf16[16,2,128]{2,1,0:T(2,128)(2,1)} reshape(bf16[16,256]{1,0:T(8,128)(2,1)S(1)} %fusion.20) | data formatting | bytes 16384 | tf_op jit(solution)/shard_map/reshape | solution.py:113
  (6 shorter events, 0.0 us)
Async XLA Ops:
  0.0 2.2 %copy-start.2 = (f32[2,128]{1,0:T(2,128)S(1)}, f32[2,128]{1,0:T(2,128)}, u32[]{:S(2)}) copy-start(f32[2,128]{1,0:T(2,128)} %param.5) | copy-start | bytes 3076
  2.3 19.5 %copy-start = (bf16[2,128,256]{2,1,0:T(8,128)(2,1)S(1)}, bf16[2,128,256]{2,1,0:T(8,128)(2,1)}, u32[]{:S(2)}) copy-start(bf16[2,128,256]{2,1,0:T(8,128)(2,1)} %param.6) | copy-start | bytes 393220
  43.0 0.7 %copy-start.1 = (s32[32,32]{1,0:T(8,128)S(1)}, s32[32,32]{1,0:T(8,128)}, u32[]{:S(2)}) copy-start(s32[32,32]{1,0:T(8,128)} %param.7) | copy-start | bytes 12292
where the time goes:
time: 48.4 us; the launch traced here: 48.1 us
  blocking collectives  45.5 us (94%)
  local copies, waits for them, and re-layouts  0.88 us (2%)
  other arithmetic  0.87 us (2%)
  matrix products  0.77 us (2%)
    all_gather x1, blocking collectives, body(): lax.all_gather(band_feats, 'row', axis=1, tiled=True)  15.9 us
    all_gather x1, blocking collectives, body(): lax.all_gather(band_belief, 'row', axis=1, tiled=True)  14 us
    all_gather x1, blocking collectives, body(): lax.all_gather(key_belief, 'col', axis=1, tiled=True)  5.13 us
    all_gather x1, blocking collectives, body(): lax.all_gather(key_feats, 'col', axis=1, tiled=True)  4.93 us
    psum x1, blocking collectives, body(): pairwise = lax.psum(partial_value, 'cls')  3.41 us
    all_gather x1, blocking collectives, body(): whole_unary = lax.all_gather(unary_scores, 'cls', axis=0, tiled=True)  2.19 us

commit v1 on v0

--- a/solution.py
+++ b/solution.py
@@ -7,6 +7,27 @@
 unit_scale = 1.0 / 64.0
 masked_low = -1e30
 key_block = 1024
+
+
+def collect(value, axis, dim):
+    length, position, span = (lax.axis_size(axis), lax.axis_index(axis), value.shape[dim])
+    right = [(i, (i + 1) % length) for i in range(length)]
+    downward = [(i, (i - 1) % length) for i in range(length)]
+    result = jnp.zeros((*value.shape[:dim], length * span, *value.shape[dim + 1 :]), value.dtype)
+    result = lax.dynamic_update_slice_in_dim(result, value, position * span, axis=dim)
+    from_left = from_right = value
+    middle = length // 2
+    for step in range(1, middle + 1):
+        from_left = lax.ppermute(from_left, axis, right)
+        result = lax.dynamic_update_slice_in_dim(
+            result, from_left, (position - step) % length * span, axis=dim
+        )
+        if step < length - middle:
+            from_right = lax.ppermute(from_right, axis, downward)
+            result = lax.dynamic_update_slice_in_dim(
+                result, from_right, (position + step) % length * span, axis=dim
+            )
+    return result
 
 
 def class_softmax(logits, live_mask):
@@ -97,10 +118,7 @@
     )
     message = fold_own(
         zero_start,
-        (
-            lax.all_gather(band_feats, "row", axis=1, tiled=True),
-            lax.all_gather(band_belief, "row", axis=1, tiled=True),
-        ),
+        (lax.all_gather(band_feats, "row", axis=1, tiled=True), collect(band_belief, "row", 1)),
         jnp.int32(0),
     )
     message = message / (2.0 * pixels)

time: 48.4 us -> 43.9 us (0.907)
  blocking collectives: 45.5 us -> 31.1 us
  waiting for transfers between devices: 0 us -> 5.29 us
  starting transfers between devices: 0 us -> 4.47 us
    all_gather x1 -> x0, blocking collectives: 14 us -> none  [body(): lax.all_gather(band_belief, 'row', axis=1, tiled=True)]
    ppermute x0 -> x3, waiting for transfers between devices: none -> 5.29 us  [the longest x2 5.28 us: collect(): from_left = lax.ppermute(from_left, axis, right)]
    ppermute x0 -> x3, starting transfers between devices: none -> 4.47 us  [the longest x2 2.42 us: collect(): from_left = lax.ppermute(from_left, axis, right)]
    all_gather x1, blocking collectives: 15.9 us -> 15.4 us  [body(): lax.all_gather(band_feats, 'row', axis=1, tiled=True)]
  transfers between devices with their start and end apart: 0 -> 3, of which waited for: 0 -> 1; matrix products, arithmetic and copies ran while one was open for 0% -> 1% of each run, Pallas kernels for 0% -> 0%
where the time goes in v1:
time: 43.9 us; the launch traced here: 43.6 us
  blocking collectives  31.1 us (71%)
  waiting for transfers between devices  5.29 us (12%)
  starting transfers between devices  4.47 us (10%)
  local copies, waits for them, and re-layouts  0.93 us (2%)
  other arithmetic  0.87 us (2%)
  matrix products  0.76 us (2%)
    all_gather x1, blocking collectives, body(): lax.all_gather(band_feats, 'row', axis=1, tiled=True)  15.4 us
    ppermute x2, waiting for transfers between devices, collect(): from_left = lax.ppermute(from_left, axis, right)  5.28 us
    all_gather x1, blocking collectives, body(): lax.all_gather(key_belief, 'col', axis=1, tiled=True)  5.14 us
    all_gather x1, blocking collectives, body(): lax.all_gather(key_feats, 'col', axis=1, tiled=True)  4.93 us
    psum x1, blocking collectives, body(): pairwise = lax.psum(partial_value, 'cls')  3.41 us
    ppermute x2, starting transfers between devices, collect(): from_left = lax.ppermute(from_left, axis, right)  2.42 us
    all_gather x1, blocking collectives, body(): whole_unary = lax.all_gather(unary_scores, 'cls', axis=0, tiled=True)  2.19 us
    ppermute x1, starting transfers between devices, collect(): from_right = lax.ppermute(from_right, axis, downward)  2.05 us
  transfers between devices with their start and end apart: 3, of which 1 were waited for; matrix products, arithmetic and copies ran while one was open for 1% of the time, Pallas kernels for 0%

profile of v1, /device:TPU:0, one launch (start us, length us, event | category | flops | bytes accessed | tf_op | source)
XLA Modules:
  0.0 43.6 jit_solution(15848004140621970318)
XLA Ops:
  0.0 0.0 copy-start.2
  0.0 2.2 %all_gather.12 = s32[32,2,128]{2,1,0:T(2,128)S(1)} all-gather(s32[16,2,128]{2,1,0:T(2,128)} %param.4), channel_id=1, replica_groups=mesh['grp'=2,'row'=4,'col'=2,'cls'=2] {'cls'}, dimensions={0}, use_global_device_ids=true | all-gather | bytes 49152 | tf_op jit(solution)/shard_map/all_gather | solution.py:84
  2.2 0.0 copy-done.2
  2.2 0.0 copy-start
  2.2 0.1 select_reduce_fusion.1
  2.3 0.1 fusion.67
  2.4 0.1 constant_dynamic-slice_fusion.1
  2.5 0.1 fusion.19
  2.6 0.1 reshape.136
  2.7 5.1 %all_gather.13 = bf16[32,256]{1,0:T(8,128)(2,1)S(1)} all-gather(bf16[32,128]{1,0:T(8,128)(2,1)S(1)} %reshape.136), channel_id=1, replica_groups=mesh['grp'=2,'row'=4,'col'=2,'cls'=2] {'col'}, dimensions={1}, use_global_device_ids=true | all-gather | bytes 24576 | tf_op jit(solution)/shard_map/all_gather | solution.py:117
  7.8 2.1 %collective-permute-start = (bf16[32,256]{1,0:T(8,128)(2,1)S(1)}, bf16[32,256]{1,0:T(8,128)(2,1)S(1)}, u32[]{:S(2)}, u32[]{:S(2)}) collective-permute-start(bf16[32,256]{1,0:T(8,128)(2,1)S(1)} %all_gather.13), channel_id=1, source_target_pairs={{0,4},{4,8},{8,12},{12,0},{1,5},{5,9},{9,13},{13,1},{2,6},{6,10},{... | collective-permute-start | bytes 49160 | tf_op jit(solution)/shard_map/ppermute | solution.py:21
  10.0 2.1 %collective-permute-start.1 = (bf16[32,256]{1,0:T(8,128)(2,1)S(1)}, bf16[32,256]{1,0:T(8,128)(2,1)S(1)}, u32[]{:S(2)}, u32[]{:S(2)}) collective-permute-start(bf16[32,256]{1,0:T(8,128)(2,1)S(1)} %all_gather.13), channel_id=1, source_target_pairs={{0,12},{4,0},{8,4},{12,8},{1,13},{5,1},{9,5},{13,9},{2,14},{6,2},{... | collective-permute-start | bytes 49160 | tf_op jit(solution)/shard_map/ppermute | solution.py:26
  12.0 0.0 copy-done
  12.1 0.1 multiply_reduce_fusion.1
  12.2 4.9 %all_gather.14 = bf16[256,256]{0,1:T(8,128)(2,1)S(1)} all-gather(bf16[256,128]{0,1:T(8,128)(2,1)S(1)} %bitcast.38), channel_id=1, replica_groups=mesh['grp'=2,'row'=4,'col'=2,'cls'=2] {'col'}, dimensions={1}, use_global_device_ids=true | all-gather | bytes 196608 | tf_op jit(solution)/shard_map/all_gather | solution.py:116
  17.1 15.4 %all_gather.15 = bf16[256,1024]{0,1:T(8,128)(2,1)S(1)} all-gather(bf16[256,256]{0,1:T(8,128)(2,1)S(1)} %all_gather.14), channel_id=1, replica_groups=mesh['grp'=2,'row'=4,'col'=2,'cls'=2] {'row'}, dimensions={1}, use_global_device_ids=true | all-gather | bytes 655360 | tf_op jit(solution)/shard_map/all_gather | solution.py:121
  32.5 0.2 multiply_reduce_fusion
  32.8 0.0 collective-permute-done
  32.9 0.3 collective-permute-start.2
  33.2 0.0 collective-permute-done.1
  33.2 5.3 %collective-permute-done.2 = bf16[32,256]{1,0:T(8,128)(2,1)S(1)} collective-permute-done((bf16[32,256]{1,0:T(8,128)(2,1)S(1)}, bf16[32,256]{1,0:T(8,128)(2,1)S(1)}, u32[]{:S(2)}, u32[]{:S(2)}) %collective-permute-start.2) | collective-permute-done | bytes 16416 | tf_op jit(solution)/shard_map/ppermute | solution.py:21
  38.4 0.0 copy-start.1
  38.4 0.6 %fusion.8 = f32[32,256]{1,0:T(8,128)S(1)} fusion(bf16[32,1024]{1,0:T(8,128)(2,1)S(1)} %constant_dynamic-update-slice_fusion, bf16[256,1024]{0,1:T(8,128)(2,1)S(1)} %all_gather.15, bf16[256,256]{1,0:T(8,128)(2,1)S(1)} %bitcast.37, f32[1024]{0:T(1024)S(1)} %multiply_reduce_fusion, f32[256]{0:T(256)S(1)} %bitcast.39, s32[1024]{0:T(1024)S(1)} %fusion.36, ...), kind=kOutput, calls=%fused_computation.9 | convolution fusion | flops 153100288 | bytes 763904 | tf_op jit(solution)/shard_map/dot_general | solution.py:48
  39.1 0.1 copy-done.1
  39.2 0.2 fusion.21
  39.3 3.4 %psum.7 = f32[32,256]{1,0:T(8,128)S(1)} all-reduce(f32[32,256]{1,0:T(8,128)S(1)} %fusion.21), channel_id=1, replica_groups=mesh['grp'=2,'row'=4,'col'=2,'cls'=2] {'cls'}, use_global_device_ids=true, to_apply=%region_4.5 | all-reduce | flops 8192 | bytes 65536 | tf_op jit(solution)/shard_map/psum | solution.py:127
  42.7 0.1 select_reduce_fusion
  42.8 0.1 fusion.66
  42.9 0.6 %reshape.139 = bf16[16,2,128]{2,1,0:T(2,128)(2,1)} reshape(bf16[16,256]{1,0:T(8,128)(2,1)S(1)} %fusion.20) | data formatting | bytes 16384 | tf_op jit(solution)/shard_map/reshape | solution.py:131
  (11 shorter events, 0.1 us)
Async XLA Ops:
  0.0 2.2 %copy-start.2 = (f32[2,128]{1,0:T(2,128)S(1)}, f32[2,128]{1,0:T(2,128)}, u32[]{:S(2)}) copy-start(f32[2,128]{1,0:T(2,128)} %param.5) | copy-start | bytes 3076
  2.2 9.8 %copy-start = (bf16[2,128,256]{2,1,0:T(8,128)(2,1)S(1)}, bf16[2,128,256]{2,1,0:T(8,128)(2,1)}, u32[]{:S(2)}) copy-start(bf16[2,128,256]{2,1,0:T(8,128)(2,1)} %param.6) | copy-start | bytes 393220
  7.8 25.0 %collective-permute-start = (bf16[32,256]{1,0:T(8,128)(2,1)S(1)}, bf16[32,256]{1,0:T(8,128)(2,1)S(1)}, u32[]{:S(2)}, u32[]{:S(2)}) collective-permute-start(bf16[32,256]{1,0:T(8,128)(2,1)S(1)} %all_gather.13), channel_id=1, source_target_pairs={{0,4},{4,8},{8,12},{12,0},{1,5},{5,9},{9,13},{13,1},{2,6},{6,10},{... | collective-permute-start | bytes 49160 | tf_op jit(solution)/shard_map/ppermute | solution.py:21
  10.0 23.2 %collective-permute-start.1 = (bf16[32,256]{1,0:T(8,128)(2,1)S(1)}, bf16[32,256]{1,0:T(8,128)(2,1)S(1)}, u32[]{:S(2)}, u32[]{:S(2)}) collective-permute-start(bf16[32,256]{1,0:T(8,128)(2,1)S(1)} %all_gather.13), channel_id=1, source_target_pairs={{0,12},{4,0},{8,4},{12,8},{1,13},{5,1},{9,5},{13,9},{2,14},{6,2},{... | collective-permute-start | bytes 49160 | tf_op jit(solution)/shard_map/ppermute | solution.py:26
  32.9 5.6 %collective-permute-start.2 = (bf16[32,256]{1,0:T(8,128)(2,1)S(1)}, bf16[32,256]{1,0:T(8,128)(2,1)S(1)}, u32[]{:S(2)}, u32[]{:S(2)}) collective-permute-start(bf16[32,256]{1,0:T(8,128)(2,1)S(1)} %collective-permute-done), channel_id=1, source_target_pairs={{0,4},{4,8},{8,12},{12,0},{1,5},{5,9},{9,13},{13,1},{2,6},{6,10},{... | collective-permute-start | bytes 49160 | tf_op jit(solution)/shard_map/ppermute | solution.py:21
  38.4 0.7 %copy-start.1 = (s32[32,32]{1,0:T(8,128)S(1)}, s32[32,32]{1,0:T(8,128)}, u32[]{:S(2)}) copy-start(s32[32,32]{1,0:T(8,128)} %param.7) | copy-start | bytes 12292
